TPU v7x, 32 devices: a 4x4x1 block of a 4x4x8 slice. The times are simulated.
32 devices in a mesh: layer: 1 (over z), col: 4 (over y), row: 8 (over x, core).
Axes of the slice: x: 4, y: 4, z: 1, core: 2. Of those that a mesh axis runs over, the one named last changes fastest.
The devices are a block of a 4x4x8 slice.
Arguments:
- weight: float32 [1024, 4096], P(('layer', 'row'), 'col')
- grad_in: float32 [1024, 4096], P(('layer', 'row'), 'col')
- mom_first: float32 [1024, 4096], P(('layer', 'row'), 'col')
- mom_second: float32 [1024, 4096], P(('layer', 'row'), 'col')
- stat_left: float32 [1024, 1024], P(('layer', 'row'), 'col')
- stat_right: float32 [4096, 4096], P(('layer', 'row'), 'col')
- basis_left: float32 [1024, 1024], P(('layer', 'row'), 'col')
- basis_right: float32 [4096, 4096], P(('layer', 'row'), 'col')
Outputs:
- output 1: float32 [1024, 4096], P(('layer', 'row'), 'col')
- output 2: float32 [1024, 4096], P(('layer', 'row'), 'col')
- output 3: float32 [1024, 4096], P(('layer', 'row'), 'col')
- output 4: float32 [1024, 1024], P(('layer', 'row'), 'col')
- output 5: float32 [4096, 4096], P(('layer', 'row'), 'col')
All inputs are finite; a program needn't handle non-finite values.
Results may differ from a plain program's by a relative error of at most 0.001.
Values are sent between devices in bfloat16 or wider.
A program may use at most 768 MiB of HBM per device.

v0:
```python
import jax
import jax.numpy as jnp
from jax import lax
from jax.sharding import PartitionSpec as P

BETA1 = 0.9
BETA2 = 0.9
EPS = 1e-8
LR = 0.1
STEP = 10
BIAS_ONE = 1.0 - BETA1 ** STEP
BIAS_TWO = 1.0 - BETA2 ** STEP


def solution(mesh):
    tile_spec = P(("layer", "row"), "col")
    highest = lax.Precision.HIGHEST
    contract_rows = (((0,), (0,)), ((), ()))
    contract_cols = (((1,), (1,)), ((), ()))

    def local_step(weight, grad_in, mom_first, mom_second, stat_left, stat_right, basis_left, basis_right):
        grad_rows = lax.all_gather(grad_in, "col", axis=1, tiled=True)
        grad_cols = lax.all_gather(grad_in, "row", axis=0, tiled=True)
        left_part = lax.dot_general(grad_in, grad_cols, contract_cols, precision=highest, preferred_element_type=jnp.float32)
        left_sum = lax.psum_scatter(left_part, "col", scatter_dimension=1, tiled=True)
        right_part = lax.dot_general(grad_rows, grad_in, contract_rows, precision=highest, preferred_element_type=jnp.float32)
        right_sum = lax.psum_scatter(right_part, "row", scatter_dimension=0, tiled=True)
        new_left = BETA2 * stat_left + (1.0 - BETA2) * left_sum
        new_right = BETA2 * stat_right + (1.0 - BETA2) * right_sum
        left_rows = lax.all_gather(basis_left.astype(jnp.bfloat16), "col", axis=1, tiled=True)
        right_cols = lax.all_gather(basis_right.astype(jnp.bfloat16), "row", axis=0, tiled=True)
        inner_rot = jnp.dot(grad_rows.astype(jnp.bfloat16), right_cols, preferred_element_type=jnp.float32).astype(jnp.bfloat16)
        rotated_part = lax.dot_general(left_rows, inner_rot, contract_rows, preferred_element_type=jnp.float32)
        rotated = lax.psum_scatter(rotated_part, "row", scatter_dimension=0, tiled=True)
        new_first = BETA1 * mom_first + (1.0 - BETA1) * rotated
        new_second = BETA2 * mom_second + (1.0 - BETA2) * rotated * rotated
        direction = (new_first / BIAS_ONE) / (jnp.sqrt(new_second / BIAS_TWO) + EPS)
        direction_cols = lax.all_gather(direction.astype(jnp.bfloat16), "row", axis=0, tiled=True)
        back_inner = jnp.dot(left_rows, direction_cols, preferred_element_type=jnp.float32).astype(jnp.bfloat16)
        update_part = lax.dot_general(back_inner, right_cols, contract_cols, preferred_element_type=jnp.float32)
        step_update = lax.psum_scatter(update_part, "col", scatter_dimension=1, tiled=True)
        new_weight = weight - LR * step_update
        return new_weight, new_first, new_second, new_left, new_right

    return jax.shard_map(local_step, mesh=mesh, in_specs=(tile_spec,) * 8, out_specs=(tile_spec,) * 5, check_vma=False)
```

profile of v0, /device:TPU:97, one launch (start us, length us, event | category | flops | bytes accessed | tf_op | source)
XLA Modules:
  0.0 344.0 jit_solution(6510761863112262761)
XLA Ops:
  7.2 0.7 all-gather.5.cloned.1.call-update
  8.1 2.7 convert_element_type.20
  10.9 12.9 %all_gather.17 = bf16[128,1024]{1,0:T(8,128)(2,1)S(1)} all-gather(bf16[128,256]{1,0:T(8,128)(2,1)S(1)} %convert_element_type.22), channel_id=1, replica_groups=mesh['layer'=1,'col'=4,'row'=8] {'col'}, dimensions={1}, use_global_device_ids=true | all-gather | bytes 327680 | tf_op jit(solution)/shard_map/all_gather | solution.py:30
  23.8 17.8 %all-gather.5.cloned.1.call-done = f32[128,4096]{1,0:T(8,128)} async-done(((f32[128,1024]{1,0:T(8,128)}), f32[128,4096]{1,0:T(8,128)}) %all-gather.5.cloned.1.call-update) | async-done | bytes 2097168 | tf_op jit(solution)/shard_map/all_gather | solution.py:22
  41.7 49.8 %all-gather.7.cloned.1.call-done = bf16[4096,1024]{1,0:T(8,128)(2,1)} async-done(((bf16[512,1024]{1,0:T(8,128)(2,1)}), bf16[4096,1024]{1,0:T(8,128)(2,1)}) %all-gather.7.cloned.1.call-update) | async-done | bytes 8388624 | tf_op jit(solution)/shard_map/all_gather | solution.py:31
  91.5 7.8 %convolution_bitcast_fusion = f32[1024,1024]{0,1:T(8,128)} fusion(bf16[128,1024]{1,0:T(8,128)(2,1)S(1)} %all_gather.17, bf16[4096,1024]{1,0:T(8,128)(2,1)} %all-gather.7.cloned.1.call-done, f32[128,4096]{1,0:T(8,128)} %all-gather.5.cloned.1.call-done), kind=kOutput, calls=%fused_computation | convolution fusion | flops 1342832640 | bytes 14942208 | tf_op jit(solution)/shard_map/dot_general | solution.py:33
  99.4 0.6 all-gather.11.cloned.1.call-update
  100.7 31.1 %reduce-scatter.5.cloned.1.call-done = f32[128,1024]{0,1:T(8,128)} async-done(((f32[1024,1024]{0,1:T(8,128)}), f32[128,1024]{0,1:T(8,128)}) %reduce-scatter.5.cloned.1.call-update) | async-done | bytes 524304 | tf_op jit(solution)/shard_map/reduce_scatter | solution.py:34
  131.8 2.2 divide_convert_fusion
  134.1 30.7 %all-gather.11.cloned.1.call-done = f32[1024,1024]{1,0:T(8,128)} async-done(((f32[128,1024]{1,0:T(8,128)}), f32[1024,1024]{1,0:T(8,128)}) %all-gather.11.cloned.1.call-update) | async-done | bytes 4194320 | tf_op jit(solution)/shard_map/all_gather | solution.py:23
  164.8 7.3 %fusion.5 = f32[128,1024]{1,0:T(8,128)} fusion(f32[128,1024]{1,0:T(8,128)S(1)} %copy-done.1, f32[1024,1024]{1,0:T(8,128)} %all-gather.11.cloned.1.call-done), kind=kOutput, calls=%fused_computation.12 | convolution fusion | flops 1610612736 | bytes 5242880 | tf_op jit(solution)/shard_map/dot_general | solution.py:24
  172.3 18.3 %all-gather.9.cloned.1.call-done = bf16[1024,1024]{0,1:T(8,128)(2,1)} async-done(((bf16[128,1024]{0,1:T(8,128)(2,1)}), bf16[1024,1024]{0,1:T(8,128)(2,1)}) %all-gather.9.cloned.1.call-update) | async-done | bytes 2097168 | tf_op jit(solution)/shard_map/all_gather | solution.py:38
  190.6 9.2 %fusion.2 = f32[128,4096]{0,1:T(8,128)} fusion(bf16[4096,1024]{1,0:T(8,128)(2,1)} %all-gather.7.cloned.1.call-done, bf16[1024,1024]{0,1:T(8,128)(2,1)} %all-gather.9.cloned.1.call-done, bf16[128,1024]{1,0:T(8,128)(2,1)S(1)} %all_gather.17), kind=kOutput, calls=%fused_computation.5 | convolution fusion | flops 1342308352 | bytes 12845056 | tf_op jit(solution)/shard_map/dot_general | solution.py:40
  200.1 1.3 copy-done
  201.4 15.9 %fusion.6 = f32[4096,1024]{1,0:T(8,128)} fusion(f32[128,4096]{1,0:T(8,128)S(1)} %copy-done, f32[128,1024]{1,0:T(8,128)S(1)} %copy-done.1), kind=kOutput, calls=%fused_computation.13 | convolution fusion | flops 6442450944 | bytes 19398656 | tf_op jit(solution)/shard_map/dot_general | solution.py:26
  217.4 1.0 copy-done.6
  218.6 1.6 multiply_add_fusion.2
  220.2 1.0 copy.18
  221.2 1.0 copy.19
  222.2 20.4 %reduce-scatter.7.cloned.1.call-done = f32[128,1024]{0,1:T(8,128)} async-done(((f32[128,4096]{0,1:T(8,128)}), f32[128,1024]{0,1:T(8,128)}) %reduce-scatter.7.cloned.1.call-update) | async-done | bytes 524304 | tf_op jit(solution)/shard_map/reduce_scatter | solution.py:41
  242.6 1.1 multiply_subtract_fusion
  243.7 1.0 copy.17
  244.7 89.0 %reduce-scatter.11.cloned.1.call-done = f32[512,1024]{1,0:T(8,128)} async-done(((f32[4096,1024]{1,0:T(8,128)}), f32[512,1024]{1,0:T(8,128)}) %reduce-scatter.11.cloned.1.call-update) | async-done | bytes 2097168 | tf_op jit(solution)/shard_map/reduce_scatter | solution.py:27
  333.7 3.4 multiply_add_fusion
  (35 shorter events, 1.9 us)
Async XLA Ops:
  7.2 34.5 %all-gather.5.cloned.1.call-start = ((), (), s32[]{:S(2)}) async-start(), calls=%async_computation.4 | async-start | bytes 2621440 | tf_op jit(solution)/shard_map/all_gather | solution.py:22
  8.0 2.9 copy-start.8
  8.0 83.5 %all-gather.7.cloned.1.call-start = ((), (), s32[]{:S(2)}) async-start(), calls=%async_computation.5 | async-start | bytes 9437184 | tf_op jit(solution)/shard_map/all_gather | solution.py:31
  10.8 120.9 %reduce-scatter.5.cloned.1.call-start = ((), (), s32[]{:S(2)}) async-start(), calls=%async_computation.6 | async-start | bytes 4718592 | tf_op jit(solution)/shard_map/reduce_scatter | solution.py:34
  99.2 1.0 copy-start.4
  99.2 1.2 copy-start.5
  99.3 65.5 %all-gather.11.cloned.1.call-start = ((), (), s32[]{:S(2)}) async-start(), calls=%async_computation.9 | async-start | bytes 4718592 | tf_op jit(solution)/shard_map/all_gather | solution.py:23
  99.9 90.6 %all-gather.9.cloned.1.call-start = ((), (), s32[]{:S(2)}) async-start(), calls=%async_computation.7 | async-start | bytes 2359296 | tf_op jit(solution)/shard_map/all_gather | solution.py:38
  100.5 64.3 %copy-start.1 = (f32[128,1024]{1,0:T(8,128)S(1)}, f32[128,1024]{1,0:T(8,128)}, u32[]{:S(2)}) copy-start(f32[128,1024]{1,0:T(8,128)} %param.9) | copy-start | bytes 1572868
  134.1 84.5 %reduce-scatter.9.cloned.1.call-start = ((), (), s32[]{:S(2)}) async-start(), calls=%async_computation.10 | async-start | bytes 655360 | tf_op jit(solution)/shard_map/reduce_scatter | solution.py:25
  172.2 70.4 %reduce-scatter.7.cloned.1.call-start = ((), (), s32[]{:S(2)}) async-start(), calls=%async_computation.8 | async-start | bytes 2621440 | tf_op jit(solution)/shard_map/reduce_scatter | solution.py:41
  199.8 1.6 copy-start
  199.9 133.8 %reduce-scatter.11.cloned.1.call-start = ((), (), s32[]{:S(2)}) async-start(), calls=%async_computation.11 | async-start | bytes 18874368 | tf_op jit(solution)/shard_map/reduce_scatter | solution.py:27
  217.3 1.0 copy-start.6
  217.3 1.3 copy-start.7
  217.3 2.9 copy-start.3
  221.2 112.6 %copy-start.2 = (f32[512,1024]{1,0:T(8,128)S(1)}, f32[512,1024]{1,0:T(8,128)}, u32[]{:S(2)}) copy-start(f32[512,1024]{1,0:T(8,128)} %param.13) | copy-start | bytes 6291460
Sparse Core Ops, SparseCore 0:
  9.6 32.0 all-gather.4
  43.9 47.5 all-gather.6
  99.4 32.2 reduce-scatter.4
  133.2 31.4 all-gather.10
  166.8 23.7 all-gather.8
  193.3 17.1 reduce-scatter.8
  213.4 29.1 reduce-scatter.6
  245.0 88.7 reduce-scatter.10
where the time goes:
time: 344 us
  waiting for transfers between devices  259 us (75%)
  matrix products  40.3 us (12%)
  between operations  14.2 us (4%)
  blocking collectives  12.9 us (4%)
  other arithmetic  11 us (3%)
  local copies, waits for them, and re-layouts  6.11 us (2%)
    reduce_scatter x1, waiting for transfers between devices, local_step(): lax.psum_scatter(right_part, 'row', scatter_dimension=0, tiled=True)  89 us
    all_gather x1, waiting for transfers between devices, local_step(): lax.all_gather(basis_right.astype(jnp.bfloat16), 'row', axis=0, tiled=True)  49.8 us
    reduce_scatter x1, waiting for transfers between devices, local_step(): lax.psum_scatter(rotated_part, 'row', scatter_dimension=0, tiled=True)  31.1 us
    all_gather x1, waiting for transfers between devices, local_step(): grad_cols = lax.all_gather(grad_in, 'row', axis=0, tiled=True)  30.7 us
    reduce_scatter x1, waiting for transfers between devices, local_step(): lax.psum_scatter(update_part, 'col', scatter_dimension=1, tiled=True)  20.4 us
    all_gather x1, waiting for transfers between devices, local_step(): lax.all_gather(direction.astype(jnp.bfloat16), 'row', axis=0, tiled=True)  18.3 us
    all_gather x1, waiting for transfers between devices, local_step(): grad_rows = lax.all_gather(grad_in, 'col', axis=1, tiled=True)  17.8 us
    dot_general x1, matrix products, local_step(): lax.dot_general(grad_rows, grad_in, contract_rows, precision=highest, pre...  15.9 us
  transfers between devices with their start and end apart: 8, of which 7 were waited for; matrix products, arithmetic and copies ran while one was open for 13% of the time, Pallas kernels for 0%

commit v1 on v0

v1 whole, which is shorter than its diff:
```python
import functools

import jax
import jax.numpy as jnp
from jax import lax
from jax.experimental import pallas as pl
from jax.experimental.pallas import tpu as pltpu
from jax.sharding import PartitionSpec as P

BETA1 = 0.9
BETA2 = 0.9
EPS = 1e-8
LR = 0.1
STEP = 10
BIAS_ONE = 1.0 - BETA1 ** STEP
BIAS_TWO = 1.0 - BETA2 ** STEP
MESH = pl.DeviceIdType.MESH
HIGHEST = lax.Precision.HIGHEST
F32 = jnp.float32
BF16 = jnp.bfloat16
NN = (((1,), (0,)), ((), ()))
TN = (((0,), (0,)), ((), ()))
NT = (((1,), (1,)), ((), ()))


def dot(a, b, dims, precision=None):
    return lax.dot_general(a, b, dims, precision=precision, preferred_element_type=F32)


def kernel(nx, ny, w_ref, g_ref, m_ref, v_ref, l_ref, r_ref, ql_ref, qr_ref,
           ow_ref, om_ref, ov_ref, ol_ref, or_ref,
           qr_f, qr_b, grow, growb, ql_f, ql_row, ql_send, ql_col, gx, gy, hb, nb,
           acc, gacc, up, rin, rbuf, lp, lrecv, lx, lbuf, wbuf, mbuf, vbuf, obuf,
           send_sem, recv_sem, local_sem):
    row = lax.axis_index("row")
    col = lax.axis_index("col")
    core = lax.rem(row, 2)
    x = lax.div(row, 2)
    nrow = 2 * nx
    rb, cb = w_ref.shape
    kb = qr_ref.shape[0]
    lb = ql_ref.shape[1]
    hr = rb // 2
    qb = rb // ny

    def wrap(v, n):
        return lax.rem(v + n, n)

    x_plus = {"row": wrap(row + 2, nrow)}
    x_minus = {"row": wrap(row - 2, nrow)}
    partner = {"row": row + 1 - 2 * core}
    y_plus = {"col": wrap(col + 1, ny)}
    y_minus = {"col": wrap(col - 1, ny)}
    prow = row + 1 - 2 * core
    counts = {"remote": 0, "local": 0}
    pending = []
    local_pending = []

    def remote(src, dst, device):
        i = counts["remote"]
        counts["remote"] += 1
        return pltpu.make_async_remote_copy(
            src_ref=src, dst_ref=dst, send_sem=send_sem.at[i], recv_sem=recv_sem.at[i],
            device_id=device, device_id_type=MESH)

    def go(copy):
        copy.start()
        pending.append(copy)

    def local(src, dst):
        i = counts["local"]
        counts["local"] += 1
        copy = pltpu.make_async_copy(src, dst, local_sem.at[i])
        copy.start()
        return copy

    class Gather8:
        def __init__(self, at, own):
            lft, rgt, far = wrap(row - 2, nrow), wrap(row + 2, nrow), wrap(row + 4, nrow)
            self.a0 = remote(own(0), at(row, 0), x_plus)
            self.a1 = remote(own(1), at(row, 1), x_plus)
            self.b1 = remote(own(1), at(row, 1), x_minus)
            self.b0 = remote(own(0), at(row, 0), x_minus)
            self.p = [remote(own(h), at(row, h), partner) for h in (0, 1)]
            self.f0 = remote(at(lft, 0), at(lft, 0), x_plus)
            self.f1 = remote(at(rgt, 1), at(rgt, 1), x_minus)
            self.near = [remote(at(s, h), at(s, h), partner) for s, h in ((lft, 0), (rgt, 1), (lft, 1), (rgt, 0))]
            self.last = [remote(at(far, h), at(far, h), partner) for h in (0, 1)]

        def start(self):
            for c in (self.a0, self.b1, self.a1, self.b0, *self.p):
                go(c)

        def forward(self):
            self.a0.wait_recv()
            go(self.f0)
            go(self.near[0])
            self.b1.wait_recv()
            go(self.f1)
            go(self.near[1])

        def second(self):
            self.a1.wait_recv()
            go(self.near[2])
            self.b0.wait_recv()
            go(self.near[3])

        def third(self):
            self.f0.wait_recv()
            go(self.last[0])
            self.f1.wait_recv()
            go(self.last[1])

        def own_ready(self):
            for c in self.p:
                c.wait_recv()

        def near_ready(self):
            for c in self.near:
                c.wait_recv()

        def far_ready(self):
            for c in self.last:
                c.wait_recv()

    class Gather4:
        def __init__(self, at, own):
            lft, rgt = wrap(col - 1, ny), wrap(col + 1, ny)
            self.a0 = remote(own(0), at(col, 0), y_plus)
            self.a1 = remote(own(1), at(col, 1), y_plus)
            self.b1 = remote(own(1), at(col, 1), y_minus)
            self.b0 = remote(own(0), at(col, 0), y_minus)
            self.f0 = remote(at(lft, 0), at(lft, 0), y_plus)
            self.f1 = remote(at(rgt, 1), at(rgt, 1), y_minus)

        def start(self):
            for c in (self.a0, self.b1, self.a1, self.b0):
                go(c)

        def forward(self):
            self.a0.wait_recv()
            go(self.f0)
            self.b1.wait_recv()
            go(self.f1)

        def second(self):
            self.a1.wait_recv()
            self.b0.wait_recv()

        def third(self):
            self.f0.wait_recv()
            self.f1.wait_recv()

    def peers():
        for dx in (1, nx - 1, 2, 0):
            for dc in (0, 1):
                if dx == 0 and dc == 0:
                    continue
                px = wrap(x + dx, nx)
                pc = core if dc == 0 else 1 - core
                yield 2 * px + pc, px, pc

    load_qr = [local(qr_ref.at[pl.ds(h * kb // 2, kb // 2)], qr_f.at[h]) for h in (0, 1)]
    load_ql = local(ql_ref, ql_f)
    load_g = [local(g_ref.at[:, pl.ds(h * kb, kb)], grow.at[2 * col + h]) for h in (0, 1)]

    barrier = pltpu.get_barrier_semaphore()
    others = [r for r, _, _ in peers()]
    for r in others:
        pl.semaphore_signal(barrier, inc=1, device_id={"row": r}, device_id_type=MESH)
    for d in (y_plus, y_minus):
        pl.semaphore_signal(barrier, inc=1, device_id=d, device_id_type=MESH)

    load_ql.wait()
    ql_row[col] = ql_f[...].astype(BF16).reshape(2, hr, lb)
    for h in (0, 1):
        load_qr[h].wait()
        qr_b[row, h] = qr_f[h].astype(BF16)
    pl.semaphore_wait(barrier, len(others) + 2)

    gather_qr = Gather8(lambda s, h: qr_b.at[s, h], lambda h: qr_b.at[row, h])
    gather_qr.start()
    gather_ql = Gather4(lambda s, h: ql_row.at[s, h], lambda h: ql_row.at[col, h])
    gather_ql.start()
    for c in load_g:
        c.wait()
    gather_g = Gather4(lambda s, h: grow.at[2 * s + h], lambda h: grow.at[2 * col + h])
    gather_g.start()

    load_m = local(m_ref, mbuf)
    load_v = local(v_ref, vbuf)
    load_own = [local(g_ref.at[:, pl.ds(h * kb, kb)], gy.at[row, h]) for h in (0, 1)]
    load_w = local(w_ref, wbuf)
    load_l = local(l_ref, lbuf)
    load_r = [local(r_ref.at[:, pl.ds(h * kb, kb)], rbuf.at[h]) for h in (0, 1)]

    def cast_block(s):
        growb[s] = grow[s].astype(BF16)

    for h in (0, 1):
        cast_block(2 * col + h)

    gather_ql.forward()
    gather_ql.second()
    gather_ql.third()
    half_l = lb // 2
    for k in range(ny):
        block = ql_row[k].reshape(rb, lb)
        for h in (0, 1):
            ql_send[2 * k + h] = block[:, h * half_l:(h + 1) * half_l]
    ql_col[row] = ql_send[row]
    send_ql = []
    for r, _, _ in peers():
        c = remote(ql_send.at[r], ql_col.at[row], {"row": r})
        go(c)
        send_ql.append(c)

    lft_c, rgt_c, far_c = wrap(col - 1, ny), wrap(col + 1, ny), wrap(col + 2, ny)
    gather_g.forward()
    cast_block(2 * lft_c)
    cast_block(2 * rgt_c + 1)
    gather_qr.forward()
    gather_g.second()
    cast_block(2 * lft_c + 1)
    cast_block(2 * rgt_c)
    gather_g.third()
    cast_block(2 * far_c)
    cast_block(2 * far_c + 1)

    def piece(r):
        return grow.at[r, pl.ds(pl.multiple_of(col * qb, qb), qb)]

    gx[row, col] = grow[row, pl.ds(pl.multiple_of(col * qb, qb), qb)]
    send_gx = []
    for r, _, _ in peers():
        c = remote(piece(r), gx.at[row, col], {"row": r})
        go(c)
        send_gx.append(c)

    def add_h(cx, first=False):
        part = dot(growb[2 * cx], qr_b[2 * cx].reshape(kb, cb), NN)
        part += dot(growb[2 * cx + 1], qr_b[2 * cx + 1].reshape(kb, cb), NN)
        if first:
            acc[...] = part
        else:
            acc[...] += part

    x_lft, x_rgt, x_far = wrap(x - 1, nx), wrap(x + 1, nx), wrap(x + 2, nx)
    gather_qr.own_ready()
    add_h(x, True)
    gather_qr.second()
    gather_qr.near_ready()
    add_h(x_lft)
    add_h(x_rgt)
    gather_qr.third()
    gather_qr.far_ready()
    add_h(x_far)
    hb[row] = acc[...].astype(BF16).reshape(2, hr, cb)
    gather_h = Gather8(lambda s, h: hb.at[s, h], lambda h: hb.at[row, h])
    gather_h.start()

    for c in send_gx:
        c.wait_recv()
    gather_gx = Gather4(
        lambda s, h: gx.at[pl.ds(h * (nrow // 2), nrow // 2), s],
        lambda h: gx.at[pl.ds(h * (nrow // 2), nrow // 2), col])
    gather_gx.start()
    for c in send_ql:
        c.wait_recv()

    def add_g(cx, first=False):
        left = ql_col[pl.ds(2 * cx, 2)].reshape(2 * rb, rb)
        part = dot(left, hb[pl.ds(2 * cx, 2)].reshape(2 * rb, cb), TN)
        if first:
            gacc[...] = part
        else:
            gacc[...] += part

    gather_h.own_ready()
    add_g(x, True)
    gather_h.forward()
    gather_h.second()
    gather_h.near_ready()
    add_g(x_lft)
    add_g(x_rgt)
    gather_h.third()
    gather_h.far_ready()
    add_g(x_far)

    load_m.wait()
    load_v.wait()
    rotated = gacc[...]
    new_first = BETA1 * mbuf[...] + (1.0 - BETA1) * rotated
    new_second = BETA2 * vbuf[...] + (1.0 - BETA2) * rotated * rotated
    direction = (new_first / BIAS_ONE) / (jnp.sqrt(new_second / BIAS_TWO) + EPS)
    nb[row] = direction.astype(BF16).reshape(2, hr, cb)
    gather_n = Gather8(lambda s, h: nb.at[s, h], lambda h: nb.at[row, h])
    gather_n.start()
    mbuf[...] = new_first
    vbuf[...] = new_second
    store_m = local(mbuf, om_ref)
    store_v = local(vbuf, ov_ref)

    gather_gx.forward()
    gather_n.forward()
    gather_y = Gather8(lambda s, h: gy.at[s, h], lambda h: grow.at[2 * col + h])
    gather_y.start()

    def add_k(cx, first=False):
        part = dot(ql_row[cx].reshape(rb, lb), nb[pl.ds(2 * cx, 2)].reshape(2 * rb, cb), NN)
        if first:
            acc[...] = part
        else:
            acc[...] += part

    gather_n.own_ready()
    add_k(x, True)
    gather_n.second()
    gather_n.near_ready()
    add_k(x_lft)
    add_k(x_rgt)
    gather_n.third()
    gather_n.far_ready()
    add_k(x_far)
    back = acc[...].astype(BF16)

    def make_u(k):
        for j in range(4):
            q = qr_b[2 * k + j // 2, j % 2]
            up[k, :, :, j * (cb // 4):(j + 1) * (cb // 4)] = dot(back, q, NT).reshape(2, hr, cb // 4)

    u_far = [remote(up.at[far_c, 0], rin.at[0], y_plus), remote(up.at[far_c, 1], rin.at[1], y_minus)]
    u_half = [remote(up.at[rgt_c, 1], rin.at[2], y_plus), remote(up.at[lft_c, 0], rin.at[3], y_minus)]
    u_sum = [remote(up.at[rgt_c, 0], rin.at[4], y_plus), remote(up.at[lft_c, 1], rin.at[5], y_minus)]
    make_u(far_c)
    for c in u_far:
        go(c)
    make_u(rgt_c)
    go(u_half[0])
    make_u(lft_c)
    go(u_half[1])
    make_u(col)

    gather_gx.second()
    gather_gx.third()
    gather_y.forward()

    right_g = gx[pl.ds(2 * col, 2)].reshape(2 * rb, kb)
    for r in range(nrow):
        lp[r] = dot(gx[r].reshape(rb, kb), right_g, NT, HIGHEST)
    swap = []
    for k in range(nx):
        c = remote(lp.at[2 * k + 1 - core], lrecv.at[k], partner)
        go(c)
        swap.append(c)

    u_far[0].wait_recv()
    up[rgt_c, 0] = up[rgt_c, 0] + rin[0]
    go(u_sum[0])
    u_far[1].wait_recv()
    up[lft_c, 1] = up[lft_c, 1] + rin[1]
    go(u_sum[1])

    for c in load_own + load_r:
        c.wait()

    for k in range(nx):
        swap[k].wait_recv()
        lp[2 * k + core] = lp[2 * k + core] + lrecv[k]
    send_l = []
    for dx in (1, nx - 1, 2):
        px = wrap(x + dx, nx)
        c = remote(lp.at[2 * px + core], lx.at[x], {"row": 2 * px + core})
        go(c)
        send_l.append(c)

    def add_r(cx, first=False):
        left = gx[pl.ds(2 * cx, 2)].reshape(2 * rb, kb)

        def body(h, _):
            part = dot(left, gy[pl.ds(2 * cx, 2), h].reshape(2 * rb, kb), TN, HIGHEST)
            old = rbuf[h]
            if first:
                old = BETA2 * old
            rbuf[h] = old + (1.0 - BETA2) * part
            return 0

        lax.fori_loop(0, 2, body, 0)

    gather_y.own_ready()
    add_r(x, True)
    gather_y.second()
    gather_y.near_ready()
    add_r(x_lft)
    add_r(x_rgt)

    for c in (*u_half, *u_sum):
        c.wait_recv()
    load_w.wait()
    obuf[:hr] = wbuf[:hr] - LR * (up[col, 0] + (rin[3] + rin[4]))
    obuf[hr:] = wbuf[hr:] - LR * (up[col, 1] + (rin[2] + rin[5]))
    store_w = local(obuf, ow_ref)

    load_l.wait()
    for c in send_l:
        c.wait_recv()
    total = lp[row]
    for dx in (1, 2, 3):
        total = total + lx[wrap(x + dx, nx)]
    lbuf[...] = BETA2 * lbuf[...] + (1.0 - BETA2) * total
    store_l = local(lbuf, ol_ref)

    gather_y.third()
    gather_y.far_ready()
    add_r(x_far)
    store_r = [local(rbuf.at[h], or_ref.at[:, pl.ds(h * kb, kb)]) for h in (0, 1)]

    for c in pending:
        c.wait_send()
    for c in (store_m, store_v, store_w, store_l, *store_r):
        c.wait()


def solution(mesh):
    nx, ny = mesh.shape["row"] // 2, mesh.shape["col"]
    tile_spec = P(("layer", "row"), "col")

    def local_step(*args):
        rb, cb = args[0].shape
        kb = args[7].shape[0]
        lb = args[6].shape[1]
        hr, nr = rb // 2, 2 * nx
        vm = pltpu.VMEM
        shapes = [args[0], args[2], args[3], args[4], args[5]]
        return pl.pallas_call(
            functools.partial(kernel, nx, ny),
            out_shape=tuple(jax.ShapeDtypeStruct(s.shape, s.dtype) for s in shapes),
            in_specs=[pl.BlockSpec(memory_space=pl.ANY)] * 8,
            out_specs=tuple([pl.BlockSpec(memory_space=pl.ANY)] * 5),
            scratch_shapes=[
                vm((2, kb // 2, cb), F32),
                vm((nr, 2, kb // 2, cb), BF16),
                vm((nr, rb, kb), F32),
                vm((nr, rb, kb), BF16),
                vm((rb, lb), F32),
                vm((ny, 2, hr, lb), BF16),
                vm((nr, rb, lb // 2), BF16),
                vm((nr, rb, lb // 2), BF16),
                vm((nr, ny, rb // ny, kb), F32),
                vm((nr, 2, rb, kb), F32),
                vm((nr, 2, hr, cb), BF16),
                vm((nr, 2, hr, cb), BF16),
                vm((rb, cb), F32),
                vm((rb, cb), F32),
                vm((ny, 2, hr, cb), F32),
                vm((6, hr, cb), F32),
                vm((2, kb, kb), F32),
                vm((nr, rb, lb), F32),
                vm((nx, rb, lb), F32),
                vm((nx, rb, lb), F32),
                vm((rb, lb), F32),
                vm((rb, cb), F32),
                vm((rb, cb), F32),
                vm((rb, cb), F32),
                vm((rb, cb), F32),
                pltpu.SemaphoreType.DMA((112,)),
                pltpu.SemaphoreType.DMA((112,)),
                pltpu.SemaphoreType.DMA((24,)),
            ],
            compiler_params=pltpu.CompilerParams(
                collective_id=0, has_side_effects=True, vmem_limit_bytes=62 * 1024 * 1024),
        )(*args)

    return jax.shard_map(local_step, mesh=mesh, in_specs=(tile_spec,) * 8, out_specs=(tile_spec,) * 5, check_vma=False)
```

time: 344 us -> 112 us (0.33)
  waiting for transfers between devices: 259 us -> 0 us
  Pallas kernels: 0 us -> 103 us
  matrix products: 40.3 us -> 0 us
  between operations: 14.2 us -> 0.66 us
  blocking collectives: 12.9 us -> 0 us
  other arithmetic: 11 us -> 0 us
    reduce_scatter x4 -> x0, waiting for transfers between devices: 141 us -> none  [the longest x1 89 us: local_step(): lax.psum_scatter(right_part, 'row', scatter_dimension=0, tiled=True)]
    all_gather x4 -> x0, waiting for transfers between devices: 117 us -> none  [the longest x1 49.8 us: local_step(): lax.all_gather(basis_right.astype(jnp.bfloat16), 'row', axis=0, tiled=True)]
    pallas_call x0 -> x1, Pallas kernels: none -> 103 us  [local_step(): pl.pallas_call(functools.partial(kernel, nx, ny), out_shape=tuple((jax.Sh...]
    dot_general x4 -> x0, matrix products: 40.3 us -> none  [the longest x1 15.9 us: local_step(): lax.dot_general(grad_rows, grad_in, contract_rows, precision=highest, pre...]
    all_gather x1 -> x0, blocking collectives: 12.9 us -> none  [local_step(): lax.all_gather(basis_left.astype(jnp.bfloat16), 'col', axis=1, tiled=True)]
    convert_element_type x3 -> x0, other arithmetic: 4.97 us -> none  [the longest x1 2.73 us: local_step(): basis_right.astype(jnp.bfloat16)]
    add x2 -> x0, other arithmetic: 4.97 us -> none  [the longest x1 3.38 us: local_step(): new_right = BETA2 * stat_right + (1.0 - BETA2) * right_sum]
    unnamed x24 -> x9, local copies, waits for them, and re-layouts: 6.11 us -> 7.79 us
  transfers between devices with their start and end apart: 8 -> 0, of which waited for: 7 -> 0; matrix products, arithmetic and copies ran while one was open for 13% -> 0% of each run, Pallas kernels for 0% -> 0%
where the time goes in v1:
time: 112 us
  Pallas kernels  103 us (92%)
  local copies, waits for them, and re-layouts  7.79 us (7%)
    pallas_call x1, Pallas kernels, local_step(): pl.pallas_call(functools.partial(kernel, nx, ny), out_shape=tuple((jax.Sh...  103 us
    unnamed x9, local copies, waits for them, and re-layouts  7.79 us

profile of v1, /device:TPU:97, one launch (start us, length us, event | category | flops | bytes accessed | tf_op | source)
XLA Modules:
  0.0 111.7 jit_solution(6545160419181283855)
XLA Ops:
  0.6 103.3 %shard_map.119 = (f32[128,1024]{1,0:T(8,128)}, f32[128,1024]{1,0:T(8,128)}, f32[128,1024]{1,0:T(8,128)}, f32[128,256]{1,0:T(8,128)}, f32[512,1024]{1,0:T(8,128)}) custom-call(f32[128,1024]{1,0:T(8,128)} %w_ref.1, f32[128,1024]{1,0:T(8,128)} %g_ref.1, f32[128,1024]{1,0:T(8,128)} %m_ref.1, f32[128,1024]{1,0:T(8,128)} %v_ref.1, f32[128,256]{1,0:T(8,128)} %l_ref.1, ...), custom_call_target="tpu_custom_call" | custom-call | tf_op jit(solution)/shard_map/pallas_call | solution.py:435
  103.9 0.0 copy-start.1
  103.9 0.0 copy-start
  103.9 2.0 %copy.18 = f32[128,1024]{1,0:T(8,128)} copy(f32[128,1024]{1,0:T(8,128)} %get-tuple-element.10) | data formatting | bytes 1048576
  106.0 1.9 %copy.19 = f32[128,1024]{1,0:T(8,128)} copy(f32[128,1024]{1,0:T(8,128)} %get-tuple-element.11) | data formatting | bytes 1048576
  107.9 1.9 %copy.20 = f32[128,1024]{1,0:T(8,128)} copy(f32[128,1024]{1,0:T(8,128)} %get-tuple-element.12) | data formatting | bytes 1048576
  109.7 0.0 copy-done.1
  109.7 0.7 copy.21
  110.4 0.0 copy-done
  110.4 1.3 %copy.22 = f32[512,1024]{1,0:T(8,128)} copy(f32[512,1024]{1,0:T(8,128)S(1)} %copy-done) | data formatting | bytes 4194304
Async XLA Ops:
  103.9 5.8 %copy-start.1 = (f32[128,256]{1,0:T(8,128)S(1)}, f32[128,256]{1,0:T(8,128)}, u32[]{:S(2)}) copy-start(f32[128,256]{1,0:T(8,128)} %get-tuple-element.13) | copy-start | bytes 393220
  103.9 6.5 %copy-start = (f32[512,1024]{1,0:T(8,128)S(1)}, f32[512,1024]{1,0:T(8,128)}, u32[]{:S(2)}) copy-start(f32[512,1024]{1,0:T(8,128)} %get-tuple-element.14) | copy-start | bytes 6291460
